TPU v7x, 32 devices: a whole 2x2x4 slice. The times are simulated.
32 devices in a mesh: mkt: 8 (over y, x, core), trade: 1, scen: 4 (over z).
Axes of the slice: x: 2, y: 2, z: 4, core: 2. Of those that a mesh axis runs over, the one named last changes fastest.
Arguments:
- quotes: bfloat16 [512, 512], P('mkt'), may hold values from -6 to 6
- kernel: bfloat16 [64, 128, 128], P(('trade', 'scen')), may hold values from -0.5 to 0.5
- trade_block: int32 [2048], P('trade'), may hold values from 0 to 63
- trade_embed: bfloat16 [2048, 256], P('trade'), may hold values from -6 to 6
- position: float32 [2048], P('trade'), may hold values from -0.125 to 0.125
- scen_rank: int32 [512], P(('mkt', 'scen')), may hold values from 0 to 511, each once
- w_in: bfloat16 [128, 256], replicated, may hold values from -0.5 to 0.5
- w_mid: bfloat16 [256, 256], replicated, may hold values from -0.375 to 0.375
- b_mid: float32 [256], replicated, may hold values from -6 to 6
- w_out: bfloat16 [256], replicated, may hold values from -0.375 to 0.375
Outputs:
- book_pnl: float32 [512], P(('mkt', 'scen'))
- marginal: float32 [2048], P('trade')
- shortfall: float32 [], replicated
Inputs may be any that keep to these rules, and one draw needn't show every extreme that they name: scen_rank holds each rank of 0 to 511 once.
All inputs are finite; a program needn't handle non-finite values.
Results may differ from a plain program's by a relative error of at most 0.014.
The roundings to bfloat16 on the way count: a program that leaves them out, or rounds other values in their place, can miss the bound.
Values may be sent and summed in bfloat16 or wider, within the bound.
No kernel may reach another device: no remote copies, remote signals or barrier semaphores. Data moves between devices by JAX's collectives and lax.ppermute only.
A program may use at most 64 MiB of HBM per device.

v0:
```python
import jax
import jax.numpy as jnp
from jax import lax
from jax.sharding import PartitionSpec as P

SEG = 128
WIN = 128
QSTEP = 8


def local(quotes, kernel, trade_block, trade_embed, position, scen_rank, w_in, w_mid, b_mid, w_out):
    local_count = kernel.shape[0]
    quote_count = quotes.shape[1]
    row_count = quotes.shape[0]
    first_block = lax.axis_index(("trade", "scen")) * local_count

    def cut_window(local_block):
        block_index = first_block + local_block
        window_start = jnp.clip(QSTEP * block_index - (WIN - QSTEP) // 2, 0, quote_count - WIN)
        return lax.dynamic_slice_in_dim(quotes, window_start, WIN, 1)

    windows = jax.vmap(cut_window)(jnp.arange(local_count, dtype=jnp.int32))
    built_state = jnp.einsum("jrw,jws->jrs", windows, kernel, preferred_element_type=jnp.float32)
    built_state = built_state.astype(jnp.bfloat16).reshape(local_count, row_count * SEG)
    scen_count = scen_rank.shape[0]
    quarter = lax.all_to_all(built_state, "scen", split_axis=1, concat_axis=0, tiled=True)
    table = lax.all_gather(quarter, "trade", axis=0, tiled=True)
    trade_rows_all = table[trade_block]
    embed_float = trade_embed.astype(jnp.float32)

    def price(scen_index):
        trade_rows = lax.dynamic_slice_in_dim(trade_rows_all, scen_index * SEG, SEG, 1)
        hidden_one = jax.nn.silu(
            jnp.dot(trade_rows, w_in, preferred_element_type=jnp.float32) + embed_float
        ).astype(jnp.bfloat16)
        hidden_two = jax.nn.silu(
            jnp.dot(hidden_one, w_mid, preferred_element_type=jnp.float32) + b_mid
        ).astype(jnp.bfloat16)
        return jnp.dot(hidden_two, w_out, preferred_element_type=jnp.float32)

    values = lax.map(price, jnp.arange(scen_count, dtype=jnp.int32))
    scen_total = scen_count * lax.axis_size("mkt") * lax.axis_size("scen")
    decay_span = scen_total // 20
    weight_sum = jnp.sum(jnp.exp(-jnp.arange(scen_total, dtype=jnp.float32) / decay_span))
    weights = jnp.exp(-scen_rank.astype(jnp.float32) / decay_span) / weight_sum
    pnl_part = jnp.dot(values, position, precision=lax.Precision.HIGHEST)
    marginal = lax.psum(-jnp.dot(weights, values, precision=lax.Precision.HIGHEST), ("mkt", "scen"))
    book_pnl = lax.psum(pnl_part, "trade")
    local_tail = -jnp.dot(weights, book_pnl, precision=lax.Precision.HIGHEST)
    shortfall = lax.psum(local_tail, ("mkt", "scen"))
    return (book_pnl, marginal, shortfall)


def solution(mesh):
    placed = (
        P("mkt", None),
        P(("trade", "scen"), None, None),
        P("trade"),
        P("trade", None),
        P("trade"),
        P(("mkt", "scen")),
        P(),
        P(),
        P(),
        P(),
    )
    return jax.shard_map(
        local,
        mesh=mesh,
        in_specs=placed,
        out_specs=(P(("mkt", "scen")), P("trade"), P()),
        check_vma=False,
    )
```

profile of v0, /device:TPU:0, one launch (start us, length us, event | category | flops | bytes accessed | tf_op | source)
XLA Modules:
  0.0 204.2 jit_solution(12396054698393962323)
XLA Ops:
  0.7 33.3 %while.12 = (s32[]{:T(128)}, bf16[64,512]{1,0:T(8,128)(2,1)}, s32[16,2]{0,1:T(2,128)S(1)}, bf16[16,64,128]{2,1,0:T(8,128)(2,1)S(1)}, s32[]{:T(128)}) while((s32[]{:T(128)}, bf16[64,512]{1,0:T(8,128)(2,1)}, s32[16,2]{0,1:T(2,128)S(1)}, bf16[16,64,128]{2,1,0:T(8,128)(2,1)S(1)}, s32[]{:T(128)}) %tuple.34), condition=%wide.while_cond, body=%wide.while_body.sunk | while | flops 2 | bytes 32865 | solution.py:20
  1.3 1.5 bitcast_dynamic-update-slice_fusion.2
  3.4 1.5 bitcast_dynamic-update-slice_fusion.2
  5.5 1.5 bitcast_dynamic-update-slice_fusion.2
  7.5 1.5 bitcast_dynamic-update-slice_fusion.2
  9.6 1.5 bitcast_dynamic-update-slice_fusion.2
  11.7 1.5 bitcast_dynamic-update-slice_fusion.2
  13.8 1.5 bitcast_dynamic-update-slice_fusion.2
  15.9 1.5 bitcast_dynamic-update-slice_fusion.2
  17.9 1.5 bitcast_dynamic-update-slice_fusion.2
  20.0 1.5 bitcast_dynamic-update-slice_fusion.2
  22.1 1.5 bitcast_dynamic-update-slice_fusion.2
  24.2 1.5 bitcast_dynamic-update-slice_fusion.2
  26.3 1.5 bitcast_dynamic-update-slice_fusion.2
  28.3 1.5 bitcast_dynamic-update-slice_fusion.2
  30.4 1.5 bitcast_dynamic-update-slice_fusion.2
  32.5 1.5 bitcast_dynamic-update-slice_fusion.2
  34.4 0.8 copy.14
  35.2 6.0 %all-to-all-start = ((bf16[16,4,2048]{2,0,1:T(8,128)(2,1)}), bf16[16,4,2048]{2,0,1:T(8,128)(2,1)S(1)}, u32[]{:S(2)}, u32[]{:S(2)}) async-start(bf16[16,4,2048]{2,0,1:T(8,128)(2,1)} %copy.14), calls=%async_computation | async-start | bytes 524288 | tf_op jit(solution)/shard_map/all_to_all | solution.py:26
  41.2 1.4 convert_element_type.16
  42.6 0.6 exponential_reduce_fusion
  43.2 6.9 %all-to-all-done = bf16[16,4,2048]{2,0,1:T(8,128)(2,1)S(1)} async-done(((bf16[16,4,2048]{2,0,1:T(8,128)(2,1)}), bf16[16,4,2048]{2,0,1:T(8,128)(2,1)S(1)}, u32[]{:S(2)}, u32[]{:S(2)}) %all-to-all-start) | async-done | bytes 262176 | tf_op jit(solution)/shard_map/all_to_all | solution.py:26
  50.2 11.0 %gather_fusion = bf16[2048,2048]{1,0:T(8,128)(2,1)} fusion(bf16[64,2048]{1,0:T(8,128)(2,1)S(1)} %bitcast.38, s32[2048]{0:T(1024)S(1)} %fusion.6), kind=kCustom, calls=%fused_computation | custom fusion | bytes 16785408 | tf_op jit(solution)/shard_map/gather | solution.py:28
  61.2 100.5 %while.11 = (s32[]{:T(128)}, f32[16,2048]{1,0:T(8,128)S(1)}, s32[16]{0:T(128)S(1)}, bf16[2048,2048]{1,0:T(8,128)(2,1)}, bf16[128,256]{1,0:T(8,128)(2,1)S(1)}, /*...) while((s32[]{:T(128)}, f32[16,2048]{1,0:T(8,128)S(1)}, ...), condition=%wide.region_1.2_spmd, body=%wide.region_0.1_spmd.sunk | while | flops 409993216 | bytes 4942527 | solution.py:41
  61.2 0.6 dynamic_slice.12
  62.4 2.8 %multiply_convert_fusion.3 = bf16[2048,256]{1,0:T(8,128)(2,1)} fusion(f32[2048,256]{1,0:T(8,128)S(1)} %get-tuple-element.215, bf16[128,256]{1,0:T(8,128)(2,1)S(1)} %get-tuple-element.214, bf16[2048,2048]{1,0:T(8,128)(2,1)} %get-tuple-element.213, s32[]{:T(128)S(6)} %select_n.23), kind=kOutput, calls=%fused_computation.4.clone.1 | convolution fusion | flops 137363456 | bytes 3735556 | tf_op jit(solution)/shard_map/while/body/eval_jaxpr/dot_general | solution.py:34
  65.2 2.0 %fusion.29 = f32[1,2048]{1,0:T(1,128)S(1)} fusion(bf16[256,1]{0,1:T(2,128)(2,1)S(1)} %reshape.77, bf16[2048,256]{1,0:T(8,128)(2,1)} %multiply_convert_fusion.3, bf16[256,256]{1,0:T(8,128)(2,1)S(1)} %get-tuple-element.216, f32[256]{0:T(256)S(1)} %get-tuple-element.217), kind=kOutput, calls=%fused_computation.5.clone.1 | convolution fusion | flops 272629760 | bytes 1189376 | tf_op jit(solution)/shard_map/while/body/eval_jaxpr/dot_general | solution.py:39
  68.7 2.8 %multiply_convert_fusion.3 = bf16[2048,256]{1,0:T(8,128)(2,1)} fusion(f32[2048,256]{1,0:T(8,128)S(1)} %get-tuple-element.215, bf16[128,256]{1,0:T(8,128)(2,1)S(1)} %get-tuple-element.214, bf16[2048,2048]{1,0:T(8,128)(2,1)} %get-tuple-element.213, s32[]{:T(128)S(6)} %select_n.23), kind=kOutput, calls=%fused_computation.4.clone.1 | convolution fusion | flops 137363456 | bytes 3735556 | tf_op jit(solution)/shard_map/while/body/eval_jaxpr/dot_general | solution.py:34
  71.5 2.0 %fusion.29 = f32[1,2048]{1,0:T(1,128)S(1)} fusion(bf16[256,1]{0,1:T(2,128)(2,1)S(1)} %reshape.77, bf16[2048,256]{1,0:T(8,128)(2,1)} %multiply_convert_fusion.3, bf16[256,256]{1,0:T(8,128)(2,1)S(1)} %get-tuple-element.216, f32[256]{0:T(256)S(1)} %get-tuple-element.217), kind=kOutput, calls=%fused_computation.5.clone.1 | convolution fusion | flops 272629760 | bytes 1189376 | tf_op jit(solution)/shard_map/while/body/eval_jaxpr/dot_general | solution.py:39
  75.0 2.8 %multiply_convert_fusion.3 = bf16[2048,256]{1,0:T(8,128)(2,1)} fusion(f32[2048,256]{1,0:T(8,128)S(1)} %get-tuple-element.215, bf16[128,256]{1,0:T(8,128)(2,1)S(1)} %get-tuple-element.214, bf16[2048,2048]{1,0:T(8,128)(2,1)} %get-tuple-element.213, s32[]{:T(128)S(6)} %select_n.23), kind=kOutput, calls=%fused_computation.4.clone.1 | convolution fusion | flops 137363456 | bytes 3735556 | tf_op jit(solution)/shard_map/while/body/eval_jaxpr/dot_general | solution.py:34
  77.8 2.0 %fusion.29 = f32[1,2048]{1,0:T(1,128)S(1)} fusion(bf16[256,1]{0,1:T(2,128)(2,1)S(1)} %reshape.77, bf16[2048,256]{1,0:T(8,128)(2,1)} %multiply_convert_fusion.3, bf16[256,256]{1,0:T(8,128)(2,1)S(1)} %get-tuple-element.216, f32[256]{0:T(256)S(1)} %get-tuple-element.217), kind=kOutput, calls=%fused_computation.5.clone.1 | convolution fusion | flops 272629760 | bytes 1189376 | tf_op jit(solution)/shard_map/while/body/eval_jaxpr/dot_general | solution.py:39
  81.3 2.8 %multiply_convert_fusion.3 = bf16[2048,256]{1,0:T(8,128)(2,1)} fusion(f32[2048,256]{1,0:T(8,128)S(1)} %get-tuple-element.215, bf16[128,256]{1,0:T(8,128)(2,1)S(1)} %get-tuple-element.214, bf16[2048,2048]{1,0:T(8,128)(2,1)} %get-tuple-element.213, s32[]{:T(128)S(6)} %select_n.23), kind=kOutput, calls=%fused_computation.4.clone.1 | convolution fusion | flops 137363456 | bytes 3735556 | tf_op jit(solution)/shard_map/while/body/eval_jaxpr/dot_general | solution.py:34
  84.1 2.0 %fusion.29 = f32[1,2048]{1,0:T(1,128)S(1)} fusion(bf16[256,1]{0,1:T(2,128)(2,1)S(1)} %reshape.77, bf16[2048,256]{1,0:T(8,128)(2,1)} %multiply_convert_fusion.3, bf16[256,256]{1,0:T(8,128)(2,1)S(1)} %get-tuple-element.216, f32[256]{0:T(256)S(1)} %get-tuple-element.217), kind=kOutput, calls=%fused_computation.5.clone.1 | convolution fusion | flops 272629760 | bytes 1189376 | tf_op jit(solution)/shard_map/while/body/eval_jaxpr/dot_general | solution.py:39
  86.3 0.6 dynamic_slice.12
  87.6 2.8 %multiply_convert_fusion.3 = bf16[2048,256]{1,0:T(8,128)(2,1)} fusion(f32[2048,256]{1,0:T(8,128)S(1)} %get-tuple-element.215, bf16[128,256]{1,0:T(8,128)(2,1)S(1)} %get-tuple-element.214, bf16[2048,2048]{1,0:T(8,128)(2,1)} %get-tuple-element.213, s32[]{:T(128)S(6)} %select_n.23), kind=kOutput, calls=%fused_computation.4.clone.1 | convolution fusion | flops 137363456 | bytes 3735556 | tf_op jit(solution)/shard_map/while/body/eval_jaxpr/dot_general | solution.py:34
  90.4 2.0 %fusion.29 = f32[1,2048]{1,0:T(1,128)S(1)} fusion(bf16[256,1]{0,1:T(2,128)(2,1)S(1)} %reshape.77, bf16[2048,256]{1,0:T(8,128)(2,1)} %multiply_convert_fusion.3, bf16[256,256]{1,0:T(8,128)(2,1)S(1)} %get-tuple-element.216, f32[256]{0:T(256)S(1)} %get-tuple-element.217), kind=kOutput, calls=%fused_computation.5.clone.1 | convolution fusion | flops 272629760 | bytes 1189376 | tf_op jit(solution)/shard_map/while/body/eval_jaxpr/dot_general | solution.py:39
  92.6 0.6 dynamic_slice.12
  93.8 2.8 %multiply_convert_fusion.3 = bf16[2048,256]{1,0:T(8,128)(2,1)} fusion(f32[2048,256]{1,0:T(8,128)S(1)} %get-tuple-element.215, bf16[128,256]{1,0:T(8,128)(2,1)S(1)} %get-tuple-element.214, bf16[2048,2048]{1,0:T(8,128)(2,1)} %get-tuple-element.213, s32[]{:T(128)S(6)} %select_n.23), kind=kOutput, calls=%fused_computation.4.clone.1 | convolution fusion | flops 137363456 | bytes 3735556 | tf_op jit(solution)/shard_map/while/body/eval_jaxpr/dot_general | solution.py:34
  96.6 2.0 %fusion.29 = f32[1,2048]{1,0:T(1,128)S(1)} fusion(bf16[256,1]{0,1:T(2,128)(2,1)S(1)} %reshape.77, bf16[2048,256]{1,0:T(8,128)(2,1)} %multiply_convert_fusion.3, bf16[256,256]{1,0:T(8,128)(2,1)S(1)} %get-tuple-element.216, f32[256]{0:T(256)S(1)} %get-tuple-element.217), kind=kOutput, calls=%fused_computation.5.clone.1 | convolution fusion | flops 272629760 | bytes 1189376 | tf_op jit(solution)/shard_map/while/body/eval_jaxpr/dot_general | solution.py:39
  100.1 2.8 %multiply_convert_fusion.3 = bf16[2048,256]{1,0:T(8,128)(2,1)} fusion(f32[2048,256]{1,0:T(8,128)S(1)} %get-tuple-element.215, bf16[128,256]{1,0:T(8,128)(2,1)S(1)} %get-tuple-element.214, bf16[2048,2048]{1,0:T(8,128)(2,1)} %get-tuple-element.213, s32[]{:T(128)S(6)} %select_n.23), kind=kOutput, calls=%fused_computation.4.clone.1 | convolution fusion | flops 137363456 | bytes 3735556 | tf_op jit(solution)/shard_map/while/body/eval_jaxpr/dot_general | solution.py:34
  102.9 2.0 %fusion.29 = f32[1,2048]{1,0:T(1,128)S(1)} fusion(bf16[256,1]{0,1:T(2,128)(2,1)S(1)} %reshape.77, bf16[2048,256]{1,0:T(8,128)(2,1)} %multiply_convert_fusion.3, bf16[256,256]{1,0:T(8,128)(2,1)S(1)} %get-tuple-element.216, f32[256]{0:T(256)S(1)} %get-tuple-element.217), kind=kOutput, calls=%fused_computation.5.clone.1 | convolution fusion | flops 272629760 | bytes 1189376 | tf_op jit(solution)/shard_map/while/body/eval_jaxpr/dot_general | solution.py:39
  106.4 2.8 %multiply_convert_fusion.3 = bf16[2048,256]{1,0:T(8,128)(2,1)} fusion(f32[2048,256]{1,0:T(8,128)S(1)} %get-tuple-element.215, bf16[128,256]{1,0:T(8,128)(2,1)S(1)} %get-tuple-element.214, bf16[2048,2048]{1,0:T(8,128)(2,1)} %get-tuple-element.213, s32[]{:T(128)S(6)} %select_n.23), kind=kOutput, calls=%fused_computation.4.clone.1 | convolution fusion | flops 137363456 | bytes 3735556 | tf_op jit(solution)/shard_map/while/body/eval_jaxpr/dot_general | solution.py:34
  109.2 2.0 %fusion.29 = f32[1,2048]{1,0:T(1,128)S(1)} fusion(bf16[256,1]{0,1:T(2,128)(2,1)S(1)} %reshape.77, bf16[2048,256]{1,0:T(8,128)(2,1)} %multiply_convert_fusion.3, bf16[256,256]{1,0:T(8,128)(2,1)S(1)} %get-tuple-element.216, f32[256]{0:T(256)S(1)} %get-tuple-element.217), kind=kOutput, calls=%fused_computation.5.clone.1 | convolution fusion | flops 272629760 | bytes 1189376 | tf_op jit(solution)/shard_map/while/body/eval_jaxpr/dot_general | solution.py:39
  111.4 0.6 dynamic_slice.12
  112.7 2.8 %multiply_convert_fusion.3 = bf16[2048,256]{1,0:T(8,128)(2,1)} fusion(f32[2048,256]{1,0:T(8,128)S(1)} %get-tuple-element.215, bf16[128,256]{1,0:T(8,128)(2,1)S(1)} %get-tuple-element.214, bf16[2048,2048]{1,0:T(8,128)(2,1)} %get-tuple-element.213, s32[]{:T(128)S(6)} %select_n.23), kind=kOutput, calls=%fused_computation.4.clone.1 | convolution fusion | flops 137363456 | bytes 3735556 | tf_op jit(solution)/shard_map/while/body/eval_jaxpr/dot_general | solution.py:34
  115.5 2.0 %fusion.29 = f32[1,2048]{1,0:T(1,128)S(1)} fusion(bf16[256,1]{0,1:T(2,128)(2,1)S(1)} %reshape.77, bf16[2048,256]{1,0:T(8,128)(2,1)} %multiply_convert_fusion.3, bf16[256,256]{1,0:T(8,128)(2,1)S(1)} %get-tuple-element.216, f32[256]{0:T(256)S(1)} %get-tuple-element.217), kind=kOutput, calls=%fused_computation.5.clone.1 | convolution fusion | flops 272629760 | bytes 1189376 | tf_op jit(solution)/shard_map/while/body/eval_jaxpr/dot_general | solution.py:39
  117.7 0.6 dynamic_slice.12
  119.0 2.8 %multiply_convert_fusion.3 = bf16[2048,256]{1,0:T(8,128)(2,1)} fusion(f32[2048,256]{1,0:T(8,128)S(1)} %get-tuple-element.215, bf16[128,256]{1,0:T(8,128)(2,1)S(1)} %get-tuple-element.214, bf16[2048,2048]{1,0:T(8,128)(2,1)} %get-tuple-element.213, s32[]{:T(128)S(6)} %select_n.23), kind=kOutput, calls=%fused_computation.4.clone.1 | convolution fusion | flops 137363456 | bytes 3735556 | tf_op jit(solution)/shard_map/while/body/eval_jaxpr/dot_general | solution.py:34
  121.8 2.0 %fusion.29 = f32[1,2048]{1,0:T(1,128)S(1)} fusion(bf16[256,1]{0,1:T(2,128)(2,1)S(1)} %reshape.77, bf16[2048,256]{1,0:T(8,128)(2,1)} %multiply_convert_fusion.3, bf16[256,256]{1,0:T(8,128)(2,1)S(1)} %get-tuple-element.216, f32[256]{0:T(256)S(1)} %get-tuple-element.217), kind=kOutput, calls=%fused_computation.5.clone.1 | convolution fusion | flops 272629760 | bytes 1189376 | tf_op jit(solution)/shard_map/while/body/eval_jaxpr/dot_general | solution.py:39
  125.2 2.8 %multiply_convert_fusion.3 = bf16[2048,256]{1,0:T(8,128)(2,1)} fusion(f32[2048,256]{1,0:T(8,128)S(1)} %get-tuple-element.215, bf16[128,256]{1,0:T(8,128)(2,1)S(1)} %get-tuple-element.214, bf16[2048,2048]{1,0:T(8,128)(2,1)} %get-tuple-element.213, s32[]{:T(128)S(6)} %select_n.23), kind=kOutput, calls=%fused_computation.4.clone.1 | convolution fusion | flops 137363456 | bytes 3735556 | tf_op jit(solution)/shard_map/while/body/eval_jaxpr/dot_general | solution.py:34
  128.0 2.0 %fusion.29 = f32[1,2048]{1,0:T(1,128)S(1)} fusion(bf16[256,1]{0,1:T(2,128)(2,1)S(1)} %reshape.77, bf16[2048,256]{1,0:T(8,128)(2,1)} %multiply_convert_fusion.3, bf16[256,256]{1,0:T(8,128)(2,1)S(1)} %get-tuple-element.216, f32[256]{0:T(256)S(1)} %get-tuple-element.217), kind=kOutput, calls=%fused_computation.5.clone.1 | convolution fusion | flops 272629760 | bytes 1189376 | tf_op jit(solution)/shard_map/while/body/eval_jaxpr/dot_general | solution.py:39
  131.5 2.8 %multiply_convert_fusion.3 = bf16[2048,256]{1,0:T(8,128)(2,1)} fusion(f32[2048,256]{1,0:T(8,128)S(1)} %get-tuple-element.215, bf16[128,256]{1,0:T(8,128)(2,1)S(1)} %get-tuple-element.214, bf16[2048,2048]{1,0:T(8,128)(2,1)} %get-tuple-element.213, s32[]{:T(128)S(6)} %select_n.23), kind=kOutput, calls=%fused_computation.4.clone.1 | convolution fusion | flops 137363456 | bytes 3735556 | tf_op jit(solution)/shard_map/while/body/eval_jaxpr/dot_general | solution.py:34
  134.3 2.0 %fusion.29 = f32[1,2048]{1,0:T(1,128)S(1)} fusion(bf16[256,1]{0,1:T(2,128)(2,1)S(1)} %reshape.77, bf16[2048,256]{1,0:T(8,128)(2,1)} %multiply_convert_fusion.3, bf16[256,256]{1,0:T(8,128)(2,1)S(1)} %get-tuple-element.216, f32[256]{0:T(256)S(1)} %get-tuple-element.217), kind=kOutput, calls=%fused_computation.5.clone.1 | convolution fusion | flops 272629760 | bytes 1189376 | tf_op jit(solution)/shard_map/while/body/eval_jaxpr/dot_general | solution.py:39
  137.8 2.8 %multiply_convert_fusion.3 = bf16[2048,256]{1,0:T(8,128)(2,1)} fusion(f32[2048,256]{1,0:T(8,128)S(1)} %get-tuple-element.215, bf16[128,256]{1,0:T(8,128)(2,1)S(1)} %get-tuple-element.214, bf16[2048,2048]{1,0:T(8,128)(2,1)} %get-tuple-element.213, s32[]{:T(128)S(6)} %select_n.23), kind=kOutput, calls=%fused_computation.4.clone.1 | convolution fusion | flops 137363456 | bytes 3735556 | tf_op jit(solution)/shard_map/while/body/eval_jaxpr/dot_general | solution.py:34
  140.6 2.0 %fusion.29 = f32[1,2048]{1,0:T(1,128)S(1)} fusion(bf16[256,1]{0,1:T(2,128)(2,1)S(1)} %reshape.77, bf16[2048,256]{1,0:T(8,128)(2,1)} %multiply_convert_fusion.3, bf16[256,256]{1,0:T(8,128)(2,1)S(1)} %get-tuple-element.216, f32[256]{0:T(256)S(1)} %get-tuple-element.217), kind=kOutput, calls=%fused_computation.5.clone.1 | convolution fusion | flops 272629760 | bytes 1189376 | tf_op jit(solution)/shard_map/while/body/eval_jaxpr/dot_general | solution.py:39
  144.1 2.8 %multiply_convert_fusion.3 = bf16[2048,256]{1,0:T(8,128)(2,1)} fusion(f32[2048,256]{1,0:T(8,128)S(1)} %get-tuple-element.215, bf16[128,256]{1,0:T(8,128)(2,1)S(1)} %get-tuple-element.214, bf16[2048,2048]{1,0:T(8,128)(2,1)} %get-tuple-element.213, s32[]{:T(128)S(6)} %select_n.23), kind=kOutput, calls=%fused_computation.4.clone.1 | convolution fusion | flops 137363456 | bytes 3735556 | tf_op jit(solution)/shard_map/while/body/eval_jaxpr/dot_general | solution.py:34
  146.9 2.0 %fusion.29 = f32[1,2048]{1,0:T(1,128)S(1)} fusion(bf16[256,1]{0,1:T(2,128)(2,1)S(1)} %reshape.77, bf16[2048,256]{1,0:T(8,128)(2,1)} %multiply_convert_fusion.3, bf16[256,256]{1,0:T(8,128)(2,1)S(1)} %get-tuple-element.216, f32[256]{0:T(256)S(1)} %get-tuple-element.217), kind=kOutput, calls=%fused_computation.5.clone.1 | convolution fusion | flops 272629760 | bytes 1189376 | tf_op jit(solution)/shard_map/while/body/eval_jaxpr/dot_general | solution.py:39
  150.4 2.8 %multiply_convert_fusion.3 = bf16[2048,256]{1,0:T(8,128)(2,1)} fusion(f32[2048,256]{1,0:T(8,128)S(1)} %get-tuple-element.215, bf16[128,256]{1,0:T(8,128)(2,1)S(1)} %get-tuple-element.214, bf16[2048,2048]{1,0:T(8,128)(2,1)} %get-tuple-element.213, s32[]{:T(128)S(6)} %select_n.23), kind=kOutput, calls=%fused_computation.4.clone.1 | convolution fusion | flops 137363456 | bytes 3735556 | tf_op jit(solution)/shard_map/while/body/eval_jaxpr/dot_general | solution.py:34
  153.2 2.0 %fusion.29 = f32[1,2048]{1,0:T(1,128)S(1)} fusion(bf16[256,1]{0,1:T(2,128)(2,1)S(1)} %reshape.77, bf16[2048,256]{1,0:T(8,128)(2,1)} %multiply_convert_fusion.3, bf16[256,256]{1,0:T(8,128)(2,1)S(1)} %get-tuple-element.216, f32[256]{0:T(256)S(1)} %get-tuple-element.217), kind=kOutput, calls=%fused_computation.5.clone.1 | convolution fusion | flops 272629760 | bytes 1189376 | tf_op jit(solution)/shard_map/while/body/eval_jaxpr/dot_general | solution.py:39
  156.7 2.8 %multiply_convert_fusion.3 = bf16[2048,256]{1,0:T(8,128)(2,1)} fusion(f32[2048,256]{1,0:T(8,128)S(1)} %get-tuple-element.215, bf16[128,256]{1,0:T(8,128)(2,1)S(1)} %get-tuple-element.214, bf16[2048,2048]{1,0:T(8,128)(2,1)} %get-tuple-element.213, s32[]{:T(128)S(6)} %select_n.23), kind=kOutput, calls=%fused_computation.4.clone.1 | convolution fusion | flops 137363456 | bytes 3735556 | tf_op jit(solution)/shard_map/while/body/eval_jaxpr/dot_general | solution.py:34
  159.5 2.0 %fusion.29 = f32[1,2048]{1,0:T(1,128)S(1)} fusion(bf16[256,1]{0,1:T(2,128)(2,1)S(1)} %reshape.77, bf16[2048,256]{1,0:T(8,128)(2,1)} %multiply_convert_fusion.3, bf16[256,256]{1,0:T(8,128)(2,1)S(1)} %get-tuple-element.216, f32[256]{0:T(256)S(1)} %get-tuple-element.217), kind=kOutput, calls=%fused_computation.5.clone.1 | convolution fusion | flops 272629760 | bytes 1189376 | tf_op jit(solution)/shard_map/while/body/eval_jaxpr/dot_general | solution.py:39
  161.7 0.8 fusion.7
  162.6 2.0 multiply_reduce_fusion
  165.3 39.0 %all-reduce.1 = (f32[2048]{0:T(1024)}, f32[]{:T(128)}) all-reduce(f32[2048]{0:T(1024)S(1)} %neg.21, f32[]{:T(128)S(6)} %neg.22), channel_id=1, replica_groups=mesh['mkt'=8,'trade'=1,'scen'=4] {'mkt','scen'}, use_global_device_ids=true, to_apply=%region_3.4 | all-reduce | flops 2049 | bytes 16392 | tf_op jit(solution)/shard_map/psum | solution.py:47
  (100 shorter events, 19.1 us)
Async XLA Ops:
  0.6 33.4 %copy-start = (bf16[16,128,128]{2,1,0:T(8,128)(2,1)S(1)}, bf16[16,128,128]{2,1,0:T(8,128)(2,1)}, u32[]{:S(2)}) copy-start(bf16[16,128,128]{2,1,0:T(8,128)(2,1)} %param.13) | copy-start | bytes 1572868
  34.4 8.9 %copy-start.2 = (s32[2048]{0:T(1024)S(1)}, s32[2048]{0:T(1024)}, u32[]{:S(2)}) copy-start(s32[2048]{0:T(1024)} %param.14) | copy-start | bytes 24580
  35.2 14.9 %all-to-all-start = ((bf16[16,4,2048]{2,0,1:T(8,128)(2,1)}), bf16[16,4,2048]{2,0,1:T(8,128)(2,1)S(1)}, u32[]{:S(2)}, u32[]{:S(2)}) async-start(bf16[16,4,2048]{2,0,1:T(8,128)(2,1)} %copy.14), calls=%async_computation | async-start | bytes 524288 | tf_op jit(solution)/shard_map/all_to_all | solution.py:26
  50.1 11.0 %copy-start.4 = (bf16[256,256]{1,0:T(8,128)(2,1)S(1)}, bf16[256,256]{1,0:T(8,128)(2,1)}, u32[]{:S(2)}) copy-start(bf16[256,256]{1,0:T(8,128)(2,1)} %param.19) | copy-start | bytes 393220
  50.1 11.0 %copy-start.5 = (bf16[128,256]{1,0:T(8,128)(2,1)S(1)}, bf16[128,256]{1,0:T(8,128)(2,1)}, u32[]{:S(2)}) copy-start(bf16[128,256]{1,0:T(8,128)(2,1)} %param.18) | copy-start | bytes 196612
  50.1 11.0 %copy-start.6 = (f32[256]{0:T(256)S(1)}, f32[256]{0:T(256)}, u32[]{:S(2)}) copy-start(f32[256]{0:T(256)} %param.20) | copy-start | bytes 3076
  50.2 11.0 %copy-start.7 = (bf16[256]{0:T(256)(128)(2,1)S(1)}, bf16[256]{0:T(256)(128)(2,1)}, u32[]{:S(2)}) copy-start(bf16[256]{0:T(256)(128)(2,1)} %param.21) | copy-start | bytes 1540
  61.1 100.6 %copy-start.3 = (s32[16]{0:T(128)S(1)}, s32[16]{0:T(128)}, u32[]{:S(2)}) copy-start(s32[16]{0:T(128)} %param.17) | copy-start | bytes 196
  61.2 101.4 %copy-start.1 = (f32[2048]{0:T(1024)S(1)}, f32[2048]{0:T(1024)}, u32[]{:S(2)}) copy-start(f32[2048]{0:T(1024)} %param.16) | copy-start | bytes 24580
where the time goes:
time: 207 us; the launch traced here: 204 us
  matrix products  80.6 us (39%)
  local copies, waits for them, and re-layouts  57.4 us (28%)
  blocking collectives  39 us (19%)
  loops' own time  10.9 us (5%)
  waiting for transfers between devices  6.9 us (3%)
  starting transfers between devices  6.02 us (3%)
    dot_general x16, matrix products, price(): jnp.dot(trade_rows, w_in, preferred_element_type=jnp.float32) + embed_float  44.7 us
    psum x1, blocking collectives, local(): lax.psum(-jnp.dot(weights, values, precision=lax.Precision.HIGHEST), ('mk...  39 us
    gather x48, local copies, waits for them, and re-layouts  33.3 us
    dot_general x16, matrix products, price(): return jnp.dot(hidden_two, w_out, preferred_element_type=jnp.float32)  32.7 us
    gather x1, local copies, waits for them, and re-layouts, local(): trade_rows_all = table[trade_block]  11 us
    another operation x1, loops' own time, local(): values = lax.map(price, jnp.arange(scen_count, dtype=jnp.int32))  10.9 us
    dynamic_slice x16, local copies, waits for them, and re-layouts, local(): values = lax.map(price, jnp.arange(scen_count, dtype=jnp.int32))  9.38 us
    all_to_all x1, waiting for transfers between devices, local(): lax.all_to_all(built_state, 'scen', split_axis=1, concat_axis=0, tiled=True)  6.9 us
  transfers between devices with their start and end apart: 1, of which 1 were waited for; matrix products, arithmetic and copies ran while one was open for 1% of the time, Pallas kernels for 0%

commit v1 on v0

--- a/solution.py
+++ b/solution.py
@@ -44,7 +44,9 @@
     weight_sum = jnp.sum(jnp.exp(-jnp.arange(scen_total, dtype=jnp.float32) / decay_span))
     weights = jnp.exp(-scen_rank.astype(jnp.float32) / decay_span) / weight_sum
     pnl_part = jnp.dot(values, position, precision=lax.Precision.HIGHEST)
-    marginal = lax.psum(-jnp.dot(weights, values, precision=lax.Precision.HIGHEST), ("mkt", "scen"))
+    marginal = lax.psum(
+        lax.psum(-jnp.dot(weights, values, precision=lax.Precision.HIGHEST), "scen"), "mkt"
+    )
     book_pnl = lax.psum(pnl_part, "trade")
     local_tail = -jnp.dot(weights, book_pnl, precision=lax.Precision.HIGHEST)
     shortfall = lax.psum(local_tail, ("mkt", "scen"))

time: 207 us -> 231 us (1.12)
  blocking collectives: 39 us -> 61.8 us
    psum x1 -> x3, blocking collectives: 39 us -> 61.8 us  [the longest x1 38.8 us: local(): shortfall = lax.psum(local_tail, ('mkt', 'scen'))]
where the time goes in v1:
time: 231 us; the launch traced here: 228 us
  matrix products  81 us (35%)
  blocking collectives  61.8 us (27%)
  local copies, waits for them, and re-layouts  57.4 us (25%)
  loops' own time  10.9 us (5%)
  waiting for transfers between devices  6.9 us (3%)
  starting transfers between devices  6.02 us (3%)
    dot_general x16, matrix products, price(): jnp.dot(trade_rows, w_in, preferred_element_type=jnp.float32) + embed_float  45.2 us
    psum x1, blocking collectives, local(): shortfall = lax.psum(local_tail, ('mkt', 'scen'))  38.8 us
    gather x48, local copies, waits for them, and re-layouts  33.3 us
    dot_general x16, matrix products, price(): return jnp.dot(hidden_two, w_out, preferred_element_type=jnp.float32)  32.7 us
    psum x1, blocking collectives, local(): lax.psum(lax.psum(-jnp.dot(weights, values, precision=lax.Precision.HIGHE...  12.6 us
    gather x1, local copies, waits for them, and re-layouts, local(): trade_rows_all = table[trade_block]  11 us
    another operation x1, loops' own time, local(): values = lax.map(price, jnp.arange(scen_count, dtype=jnp.int32))  10.9 us
    psum x1, blocking collectives, local(): lax.psum(-jnp.dot(weights, values, precision=lax.Precision.HIGHEST), 'scen')  10.4 us
  transfers between devices with their start and end apart: 1, of which 1 were waited for; matrix products, arithmetic and copies ran while one was open for 1% of the time, Pallas kernels for 0%

profile of v1, /device:TPU:0, one launch (start us, length us, event | category | flops | bytes accessed | tf_op | source)
XLA Modules:
  0.0 227.6 jit_solution(3356208711474794789)
XLA Ops:
  0.7 33.3 %while.12 = (s32[]{:T(128)}, bf16[64,512]{1,0:T(8,128)(2,1)}, s32[16,2]{0,1:T(2,128)S(1)}, bf16[16,64,128]{2,1,0:T(8,128)(2,1)S(1)}, s32[]{:T(128)}) while((s32[]{:T(128)}, bf16[64,512]{1,0:T(8,128)(2,1)}, s32[16,2]{0,1:T(2,128)S(1)}, bf16[16,64,128]{2,1,0:T(8,128)(2,1)S(1)}, s32[]{:T(128)}) %tuple.34), condition=%wide.while_cond, body=%wide.while_body.sunk | while | flops 2 | bytes 32865 | solution.py:20
  1.3 1.5 bitcast_dynamic-update-slice_fusion.2
  3.4 1.5 bitcast_dynamic-update-slice_fusion.2
  5.5 1.5 bitcast_dynamic-update-slice_fusion.2
  7.5 1.5 bitcast_dynamic-update-slice_fusion.2
  9.6 1.5 bitcast_dynamic-update-slice_fusion.2
  11.7 1.5 bitcast_dynamic-update-slice_fusion.2
  13.8 1.5 bitcast_dynamic-update-slice_fusion.2
  15.9 1.5 bitcast_dynamic-update-slice_fusion.2
  17.9 1.5 bitcast_dynamic-update-slice_fusion.2
  20.0 1.5 bitcast_dynamic-update-slice_fusion.2
  22.1 1.5 bitcast_dynamic-update-slice_fusion.2
  24.2 1.5 bitcast_dynamic-update-slice_fusion.2
  26.3 1.5 bitcast_dynamic-update-slice_fusion.2
  28.3 1.5 bitcast_dynamic-update-slice_fusion.2
  30.4 1.5 bitcast_dynamic-update-slice_fusion.2
  32.5 1.5 bitcast_dynamic-update-slice_fusion.2
  34.4 0.8 copy.14
  35.2 6.0 %all-to-all-start = ((bf16[16,4,2048]{2,0,1:T(8,128)(2,1)}), bf16[16,4,2048]{2,0,1:T(8,128)(2,1)S(1)}, u32[]{:S(2)}, u32[]{:S(2)}) async-start(bf16[16,4,2048]{2,0,1:T(8,128)(2,1)} %copy.14), calls=%async_computation | async-start | bytes 524288 | tf_op jit(solution)/shard_map/all_to_all | solution.py:26
  41.2 1.4 convert_element_type.16
  42.6 0.6 exponential_reduce_fusion
  43.2 6.9 %all-to-all-done = bf16[16,4,2048]{2,0,1:T(8,128)(2,1)S(1)} async-done(((bf16[16,4,2048]{2,0,1:T(8,128)(2,1)}), bf16[16,4,2048]{2,0,1:T(8,128)(2,1)S(1)}, u32[]{:S(2)}, u32[]{:S(2)}) %all-to-all-start) | async-done | bytes 262176 | tf_op jit(solution)/shard_map/all_to_all | solution.py:26
  50.2 11.0 %gather_fusion = bf16[2048,2048]{1,0:T(8,128)(2,1)} fusion(bf16[64,2048]{1,0:T(8,128)(2,1)S(1)} %bitcast.38, s32[2048]{0:T(1024)S(1)} %fusion.6), kind=kCustom, calls=%fused_computation | custom fusion | bytes 16785408 | tf_op jit(solution)/shard_map/gather | solution.py:28
  61.2 101.0 %while.11 = (s32[]{:T(128)}, f32[16,2048]{1,0:T(8,128)S(1)}, s32[16]{0:T(128)S(1)}, bf16[2048,2048]{1,0:T(8,128)(2,1)}, bf16[128,256]{1,0:T(8,128)(2,1)S(1)}, /*...) while((s32[]{:T(128)}, f32[16,2048]{1,0:T(8,128)S(1)}, ...), condition=%wide.region_1.2_spmd, body=%wide.region_0.1_spmd.sunk | while | flops 409993216 | bytes 4942527 | solution.py:41
  61.2 0.6 dynamic_slice.12
  62.5 2.8 %multiply_convert_fusion.3 = bf16[2048,256]{1,0:T(8,128)(2,1)} fusion(f32[2048,256]{1,0:T(8,128)S(1)} %get-tuple-element.213, bf16[128,256]{1,0:T(8,128)(2,1)S(1)} %get-tuple-element.212, bf16[2048,2048]{1,0:T(8,128)(2,1)} %get-tuple-element.211, s32[]{:T(128)S(6)} %select_n.23), kind=kOutput, calls=%fused_computation.4.clone.1 | convolution fusion | flops 137363456 | bytes 3735556 | tf_op jit(solution)/shard_map/while/body/eval_jaxpr/dot_general | solution.py:34
  65.3 2.0 fusion.29
  67.5 0.6 dynamic_slice.12
  68.8 2.8 %multiply_convert_fusion.3 = bf16[2048,256]{1,0:T(8,128)(2,1)} fusion(f32[2048,256]{1,0:T(8,128)S(1)} %get-tuple-element.213, bf16[128,256]{1,0:T(8,128)(2,1)S(1)} %get-tuple-element.212, bf16[2048,2048]{1,0:T(8,128)(2,1)} %get-tuple-element.211, s32[]{:T(128)S(6)} %select_n.23), kind=kOutput, calls=%fused_computation.4.clone.1 | convolution fusion | flops 137363456 | bytes 3735556 | tf_op jit(solution)/shard_map/while/body/eval_jaxpr/dot_general | solution.py:34
  71.6 2.0 fusion.29
  73.8 0.6 dynamic_slice.12
  75.1 2.8 %multiply_convert_fusion.3 = bf16[2048,256]{1,0:T(8,128)(2,1)} fusion(f32[2048,256]{1,0:T(8,128)S(1)} %get-tuple-element.213, bf16[128,256]{1,0:T(8,128)(2,1)S(1)} %get-tuple-element.212, bf16[2048,2048]{1,0:T(8,128)(2,1)} %get-tuple-element.211, s32[]{:T(128)S(6)} %select_n.23), kind=kOutput, calls=%fused_computation.4.clone.1 | convolution fusion | flops 137363456 | bytes 3735556 | tf_op jit(solution)/shard_map/while/body/eval_jaxpr/dot_general | solution.py:34
  77.9 2.0 fusion.29
  81.4 2.8 %multiply_convert_fusion.3 = bf16[2048,256]{1,0:T(8,128)(2,1)} fusion(f32[2048,256]{1,0:T(8,128)S(1)} %get-tuple-element.213, bf16[128,256]{1,0:T(8,128)(2,1)S(1)} %get-tuple-element.212, bf16[2048,2048]{1,0:T(8,128)(2,1)} %get-tuple-element.211, s32[]{:T(128)S(6)} %select_n.23), kind=kOutput, calls=%fused_computation.4.clone.1 | convolution fusion | flops 137363456 | bytes 3735556 | tf_op jit(solution)/shard_map/while/body/eval_jaxpr/dot_general | solution.py:34
  84.2 2.0 fusion.29
  87.7 2.8 %multiply_convert_fusion.3 = bf16[2048,256]{1,0:T(8,128)(2,1)} fusion(f32[2048,256]{1,0:T(8,128)S(1)} %get-tuple-element.213, bf16[128,256]{1,0:T(8,128)(2,1)S(1)} %get-tuple-element.212, bf16[2048,2048]{1,0:T(8,128)(2,1)} %get-tuple-element.211, s32[]{:T(128)S(6)} %select_n.23), kind=kOutput, calls=%fused_computation.4.clone.1 | convolution fusion | flops 137363456 | bytes 3735556 | tf_op jit(solution)/shard_map/while/body/eval_jaxpr/dot_general | solution.py:34
  90.5 2.0 fusion.29
  94.0 2.8 %multiply_convert_fusion.3 = bf16[2048,256]{1,0:T(8,128)(2,1)} fusion(f32[2048,256]{1,0:T(8,128)S(1)} %get-tuple-element.213, bf16[128,256]{1,0:T(8,128)(2,1)S(1)} %get-tuple-element.212, bf16[2048,2048]{1,0:T(8,128)(2,1)} %get-tuple-element.211, s32[]{:T(128)S(6)} %select_n.23), kind=kOutput, calls=%fused_computation.4.clone.1 | convolution fusion | flops 137363456 | bytes 3735556 | tf_op jit(solution)/shard_map/while/body/eval_jaxpr/dot_general | solution.py:34
  96.8 2.0 fusion.29
  100.3 2.8 %multiply_convert_fusion.3 = bf16[2048,256]{1,0:T(8,128)(2,1)} fusion(f32[2048,256]{1,0:T(8,128)S(1)} %get-tuple-element.213, bf16[128,256]{1,0:T(8,128)(2,1)S(1)} %get-tuple-element.212, bf16[2048,2048]{1,0:T(8,128)(2,1)} %get-tuple-element.211, s32[]{:T(128)S(6)} %select_n.23), kind=kOutput, calls=%fused_computation.4.clone.1 | convolution fusion | flops 137363456 | bytes 3735556 | tf_op jit(solution)/shard_map/while/body/eval_jaxpr/dot_general | solution.py:34
  103.2 2.0 fusion.29
  106.6 2.8 %multiply_convert_fusion.3 = bf16[2048,256]{1,0:T(8,128)(2,1)} fusion(f32[2048,256]{1,0:T(8,128)S(1)} %get-tuple-element.213, bf16[128,256]{1,0:T(8,128)(2,1)S(1)} %get-tuple-element.212, bf16[2048,2048]{1,0:T(8,128)(2,1)} %get-tuple-element.211, s32[]{:T(128)S(6)} %select_n.23), kind=kOutput, calls=%fused_computation.4.clone.1 | convolution fusion | flops 137363456 | bytes 3735556 | tf_op jit(solution)/shard_map/while/body/eval_jaxpr/dot_general | solution.py:34
  109.5 2.0 fusion.29
  113.0 2.8 %multiply_convert_fusion.3 = bf16[2048,256]{1,0:T(8,128)(2,1)} fusion(f32[2048,256]{1,0:T(8,128)S(1)} %get-tuple-element.213, bf16[128,256]{1,0:T(8,128)(2,1)S(1)} %get-tuple-element.212, bf16[2048,2048]{1,0:T(8,128)(2,1)} %get-tuple-element.211, s32[]{:T(128)S(6)} %select_n.23), kind=kOutput, calls=%fused_computation.4.clone.1 | convolution fusion | flops 137363456 | bytes 3735556 | tf_op jit(solution)/shard_map/while/body/eval_jaxpr/dot_general | solution.py:34
  115.8 2.0 fusion.29
  119.3 2.8 %multiply_convert_fusion.3 = bf16[2048,256]{1,0:T(8,128)(2,1)} fusion(f32[2048,256]{1,0:T(8,128)S(1)} %get-tuple-element.213, bf16[128,256]{1,0:T(8,128)(2,1)S(1)} %get-tuple-element.212, bf16[2048,2048]{1,0:T(8,128)(2,1)} %get-tuple-element.211, s32[]{:T(128)S(6)} %select_n.23), kind=kOutput, calls=%fused_computation.4.clone.1 | convolution fusion | flops 137363456 | bytes 3735556 | tf_op jit(solution)/shard_map/while/body/eval_jaxpr/dot_general | solution.py:34
  122.1 2.0 fusion.29
  125.6 2.8 %multiply_convert_fusion.3 = bf16[2048,256]{1,0:T(8,128)(2,1)} fusion(f32[2048,256]{1,0:T(8,128)S(1)} %get-tuple-element.213, bf16[128,256]{1,0:T(8,128)(2,1)S(1)} %get-tuple-element.212, bf16[2048,2048]{1,0:T(8,128)(2,1)} %get-tuple-element.211, s32[]{:T(128)S(6)} %select_n.23), kind=kOutput, calls=%fused_computation.4.clone.1 | convolution fusion | flops 137363456 | bytes 3735556 | tf_op jit(solution)/shard_map/while/body/eval_jaxpr/dot_general | solution.py:34
  128.4 2.0 fusion.29
  131.9 2.8 %multiply_convert_fusion.3 = bf16[2048,256]{1,0:T(8,128)(2,1)} fusion(f32[2048,256]{1,0:T(8,128)S(1)} %get-tuple-element.213, bf16[128,256]{1,0:T(8,128)(2,1)S(1)} %get-tuple-element.212, bf16[2048,2048]{1,0:T(8,128)(2,1)} %get-tuple-element.211, s32[]{:T(128)S(6)} %select_n.23), kind=kOutput, calls=%fused_computation.4.clone.1 | convolution fusion | flops 137363456 | bytes 3735556 | tf_op jit(solution)/shard_map/while/body/eval_jaxpr/dot_general | solution.py:34
  134.7 2.0 fusion.29
  138.2 2.8 %multiply_convert_fusion.3 = bf16[2048,256]{1,0:T(8,128)(2,1)} fusion(f32[2048,256]{1,0:T(8,128)S(1)} %get-tuple-element.213, bf16[128,256]{1,0:T(8,128)(2,1)S(1)} %get-tuple-element.212, bf16[2048,2048]{1,0:T(8,128)(2,1)} %get-tuple-element.211, s32[]{:T(128)S(6)} %select_n.23), kind=kOutput, calls=%fused_computation.4.clone.1 | convolution fusion | flops 137363456 | bytes 3735556 | tf_op jit(solution)/shard_map/while/body/eval_jaxpr/dot_general | solution.py:34
  141.0 2.0 fusion.29
  144.5 2.8 %multiply_convert_fusion.3 = bf16[2048,256]{1,0:T(8,128)(2,1)} fusion(f32[2048,256]{1,0:T(8,128)S(1)} %get-tuple-element.213, bf16[128,256]{1,0:T(8,128)(2,1)S(1)} %get-tuple-element.212, bf16[2048,2048]{1,0:T(8,128)(2,1)} %get-tuple-element.211, s32[]{:T(128)S(6)} %select_n.23), kind=kOutput, calls=%fused_computation.4.clone.1 | convolution fusion | flops 137363456 | bytes 3735556 | tf_op jit(solution)/shard_map/while/body/eval_jaxpr/dot_general | solution.py:34
  147.3 2.0 fusion.29
  150.8 2.8 %multiply_convert_fusion.3 = bf16[2048,256]{1,0:T(8,128)(2,1)} fusion(f32[2048,256]{1,0:T(8,128)S(1)} %get-tuple-element.213, bf16[128,256]{1,0:T(8,128)(2,1)S(1)} %get-tuple-element.212, bf16[2048,2048]{1,0:T(8,128)(2,1)} %get-tuple-element.211, s32[]{:T(128)S(6)} %select_n.23), kind=kOutput, calls=%fused_computation.4.clone.1 | convolution fusion | flops 137363456 | bytes 3735556 | tf_op jit(solution)/shard_map/while/body/eval_jaxpr/dot_general | solution.py:34
  153.6 2.0 fusion.29
  157.1 2.8 %multiply_convert_fusion.3 = bf16[2048,256]{1,0:T(8,128)(2,1)} fusion(f32[2048,256]{1,0:T(8,128)S(1)} %get-tuple-element.213, bf16[128,256]{1,0:T(8,128)(2,1)S(1)} %get-tuple-element.212, bf16[2048,2048]{1,0:T(8,128)(2,1)} %get-tuple-element.211, s32[]{:T(128)S(6)} %select_n.23), kind=kOutput, calls=%fused_computation.4.clone.1 | convolution fusion | flops 137363456 | bytes 3735556 | tf_op jit(solution)/shard_map/while/body/eval_jaxpr/dot_general | solution.py:34
  160.0 2.0 fusion.29
  162.2 2.0 multiply_reduce_fusion
  164.9 0.8 fusion.7
  165.7 38.8 %psum.26 = f32[]{:T(128)} all-reduce(f32[]{:T(128)S(6)} %neg.22), channel_id=1, replica_groups=mesh['mkt'=8,'trade'=1,'scen'=4] {'mkt','scen'}, use_global_device_ids=true, to_apply=%region_5.6 | all-reduce | flops 1 | bytes 8 | tf_op jit(solution)/shard_map/psum | solution.py:52
  204.6 10.4 %psum.24 = f32[2048]{0:T(1024)S(1)} all-reduce(f32[2048]{0:T(1024)S(1)} %neg.21), channel_id=1, replica_groups=mesh['mkt'=8,'trade'=1,'scen'=4] {'scen'}, use_global_device_ids=true, to_apply=%region_3.4 | all-reduce | flops 2048 | bytes 16384 | tf_op jit(solution)/shard_map/psum | solution.py:48
  215.0 12.6 %psum.25 = f32[2048]{0:T(1024)} all-reduce(f32[2048]{0:T(1024)S(1)} %psum.24), channel_id=1, replica_groups=mesh['mkt'=8,'trade'=1,'scen'=4] {'mkt'}, use_global_device_ids=true, to_apply=%region_4.5 | all-reduce | flops 2048 | bytes 16384 | tf_op jit(solution)/shard_map/psum | solution.py:47
  (102 shorter events, 20.2 us)
Async XLA Ops:
  0.6 33.4 %copy-start = (bf16[16,128,128]{2,1,0:T(8,128)(2,1)S(1)}, bf16[16,128,128]{2,1,0:T(8,128)(2,1)}, u32[]{:S(2)}) copy-start(bf16[16,128,128]{2,1,0:T(8,128)(2,1)} %param.13) | copy-start | bytes 1572868
  34.4 8.9 %copy-start.2 = (s32[2048]{0:T(1024)S(1)}, s32[2048]{0:T(1024)}, u32[]{:S(2)}) copy-start(s32[2048]{0:T(1024)} %param.14) | copy-start | bytes 24580
  35.2 14.9 %all-to-all-start = ((bf16[16,4,2048]{2,0,1:T(8,128)(2,1)}), bf16[16,4,2048]{2,0,1:T(8,128)(2,1)S(1)}, u32[]{:S(2)}, u32[]{:S(2)}) async-start(bf16[16,4,2048]{2,0,1:T(8,128)(2,1)} %copy.14), calls=%async_computation | async-start | bytes 524288 | tf_op jit(solution)/shard_map/all_to_all | solution.py:26
  50.1 11.0 %copy-start.4 = (bf16[256,256]{1,0:T(8,128)(2,1)S(1)}, bf16[256,256]{1,0:T(8,128)(2,1)}, u32[]{:S(2)}) copy-start(bf16[256,256]{1,0:T(8,128)(2,1)} %param.19) | copy-start | bytes 393220
  50.1 11.0 %copy-start.5 = (bf16[128,256]{1,0:T(8,128)(2,1)S(1)}, bf16[128,256]{1,0:T(8,128)(2,1)}, u32[]{:S(2)}) copy-start(bf16[128,256]{1,0:T(8,128)(2,1)} %param.18) | copy-start | bytes 196612
  50.1 11.0 %copy-start.6 = (f32[256]{0:T(256)S(1)}, f32[256]{0:T(256)}, u32[]{:S(2)}) copy-start(f32[256]{0:T(256)} %param.20) | copy-start | bytes 3076
  50.1 11.0 %copy-start.7 = (bf16[256]{0:T(256)(128)(2,1)S(1)}, bf16[256]{0:T(256)(128)(2,1)}, u32[]{:S(2)}) copy-start(bf16[256]{0:T(256)(128)(2,1)} %param.21) | copy-start | bytes 1540
  61.2 101.0 %copy-start.1 = (f32[2048]{0:T(1024)S(1)}, f32[2048]{0:T(1024)}, u32[]{:S(2)}) copy-start(f32[2048]{0:T(1024)} %param.16) | copy-start | bytes 24580
  61.2 101.0 %copy-start.3 = (s32[16]{0:T(128)S(1)}, s32[16]{0:T(128)}, u32[]{:S(2)}) copy-start(s32[16]{0:T(128)} %param.17) | copy-start | bytes 196
